TPU v7x, 32 devices: a whole 2x2x4 slice. The times are simulated.
32 devices in a mesh: query: 4 (over y, x), train: 4 (over z), mp: 2 (over core).
Axes of the slice: x: 2, y: 2, z: 4, core: 2. Of those that a mesh axis runs over, the one named last changes fastest.
Arguments:
- residual: bfloat16 [512, 8192], P('train'), may hold values from -6 to 6
- norm_gain: float32 [8192], replicated, may hold values from 0.1 to 1.9
- gate_weight: bfloat16 [8192, 14336], P('train', ('query', 'mp')), may hold values from -0.0625 to 0.0625
- up_weight: bfloat16 [8192, 14336], P('train', ('query', 'mp')), may hold values from -0.0625 to 0.0625
- out_grad: bfloat16 [512, 8192], P('train', ('query', 'mp')), may hold values from -6 to 6
- left_factor: bfloat16 [8, 32, 14336], P(('query', 'mp')), may hold values from -0.0078125 to 0.0078125
- right_factor: bfloat16 [8, 32, 8192], P(('query', 'mp')), may hold values from -0.0625 to 0.0625
Outputs:
- scores: float32 [8, 512], P(('query', 'mp'), 'train')
All inputs are finite; a program needn't handle non-finite values.
Results may differ from a plain program's by a relative error of at most 0.023.
Values may be sent and summed in bfloat16 or wider, within the bound.
A program may use at most 64 MiB of HBM per device.

v0:
```python
import jax
import jax.numpy as jnp
from jax import lax
from jax.sharding import PartitionSpec as P

norm_eps = 1e-05


def on_device(residual, norm_gain, gate_weight, up_weight, out_grad, left_factor, right_factor):
    values = residual.astype(jnp.float32)
    mean_sq = jnp.mean(values * values, axis=1, keepdims=True)
    normed = (values * lax.rsqrt(mean_sq + norm_eps) * norm_gain[None, :]).astype(jnp.bfloat16)
    tok_rows = normed.shape[0]
    hidden_cols = gate_weight.shape[1]
    all_rows = lax.all_to_all(normed, "train", split_axis=1, concat_axis=0, tiled=True)
    paired = jnp.concatenate([gate_weight, up_weight], axis=1)
    summed = lax.psum_scatter(
        jnp.dot(all_rows, paired, preferred_element_type=jnp.float32).astype(jnp.bfloat16),
        "train",
        scatter_dimension=0,
        tiled=True,
    ).astype(jnp.float32)
    activation = (jax.nn.silu(summed[:, :hidden_cols]) * summed[:, hidden_cols:]).astype(
        jnp.bfloat16
    )
    queries = left_factor.shape[0]
    factor_rank = left_factor.shape[1]
    contract = (((1,), (1,)), ((), ()))
    left_flat = left_factor.reshape(queries * factor_rank, left_factor.shape[2])
    columns = left_flat
    projected = lax.dot_general(
        columns,
        lax.all_gather(activation, ("query", "mp"), axis=1, tiled=True),
        contract,
        preferred_element_type=jnp.float32,
    )
    right_flat = right_factor.reshape(queries * factor_rank, right_factor.shape[2])
    columns = right_flat
    sensed = lax.dot_general(
        columns,
        lax.all_gather(out_grad, ("query", "mp"), axis=1, tiled=True),
        contract,
        preferred_element_type=jnp.float32,
    )
    return jnp.sum((projected * sensed).reshape(queries, factor_rank, tok_rows), axis=1)


def solution(mesh):
    placed = (
        P("train", None),
        P(),
        P("train", ("query", "mp")),
        P("train", ("query", "mp")),
        P("train", ("query", "mp")),
        P(("query", "mp"), None, None),
        P(("query", "mp"), None, None),
    )
    return jax.shard_map(
        on_device,
        mesh=mesh,
        in_specs=placed,
        out_specs=P(("query", "mp"), "train"),
        check_vma=False,
    )
```

profile of v0, /device:TPU:0, one launch (start us, length us, event | category | flops | bytes accessed | tf_op | source)
XLA Modules:
  0.0 204.0 jit_solution(16912763031052419279)
XLA Ops:
  7.4 0.0 copy-start
  7.4 0.0 copy-start.2
  7.4 0.0 reduce-scatter.2.cloned.1.call-start
  7.4 3.3 %copy.8 = bf16[128,8192]{0,1:T(8,128)(2,1)S(1)} copy(bf16[128,8192]{1,0:T(8,128)(2,1)} %param.7) | data formatting | bytes 4194304 | tf_op args[0]
  10.7 1.1 fusion.7
  11.8 0.0 copy-done.2
  11.8 3.5 %fusion.9 = bf16[128,8192]{0,1:T(8,128)(2,1)S(1)} fusion(bf16[128,8192]{0,1:T(8,128)(2,1)S(1)} %copy.8, f32[8192]{0:T(1024)S(1)} %copy-done.2, f32[128]{0:T(128)S(1)} %add_rsqrt_fusion), kind=kLoop, calls=%fused_computation.9 | loop fusion | flops 4194304 | bytes 4227584 | tf_op jit(solution)/shard_map/convert_element_type | solution.py:12
  15.3 54.3 %all_to_all.19 = bf16[128,4,2048]{0,2,1:T(8,128)(2,1)S(1)} all-to-all(bf16[128,4,2048]{0,2,1:T(8,128)(2,1)S(1)} %bitcast.19), channel_id=1, replica_groups=mesh['query'=4,'train'=4,'mp'=2] {'train'}, dimensions={1} | all-to-all | bytes 4194304 | tf_op jit(solution)/shard_map/all_to_all | solution.py:15
  69.6 2.7 %copy.9 = bf16[4,128,2048]{2,1,0:T(8,128)(2,1)} copy(bf16[4,128,2048]{1,2,0:T(8,128)(2,1)S(1)} %bitcast.20) | data formatting | bytes 4194304 | tf_op jit(solution)/shard_map/all_to_all | solution.py:15
  72.3 15.3 %fusion.4 = bf16[512,3584]{1,0:T(8,128)(2,1)} fusion(bf16[512,2048]{1,0:T(8,128)(2,1)} %bitcast.21, bf16[2048,1792]{1,0:T(8,128)(2,1)} %param.10, bf16[2048,1792]{1,0:T(8,128)(2,1)} %param.9), kind=kOutput, calls=%fused_computation.4 | convolution fusion | flops 7547387904 | bytes 20447232 | tf_op jit(solution)/shard_map/dot_general | solution.py:18
  87.6 0.0 reduce-scatter.2.cloned.1.call-update
  87.7 0.0 copy-start.1
  87.7 0.0 all-gather.5.cloned.1.call-start
  87.7 0.5 all-gather.5.cloned.1.call-update
  88.3 0.0 all-gather.3.cloned.1.call-start
  88.3 67.3 %reduce-scatter.2.cloned.1.call-done = bf16[128,3584]{1,0:T(8,128)(2,1)} async-done(((bf16[512,3584]{1,0:T(8,128)(2,1)}), bf16[128,3584]{1,0:T(8,128)(2,1)}) %reduce-scatter.2.cloned.1.call-update) | async-done | bytes 917520 | tf_op jit(solution)/shard_map/reduce_scatter | solution.py:17
  155.6 1.4 convert_element_type.18
  157.0 1.0 fusion.12
  158.0 0.0 all-gather.3.cloned.1.call-update
  158.0 0.0 all-gather.5.cloned.1.call-done
  158.1 0.0 copy-done.1
  158.1 2.4 %fusion.14 = f32[32,128]{1,0:T(8,128)S(1)} fusion(bf16[128,8192]{1,0:T(8,128)(2,1)} %all-gather.5.cloned.1.call-done, bf16[1,32,8192]{2,1,0:T(8,128)(2,1)S(1)} %copy-done.1), kind=kOutput, calls=%fused_computation.16 | convolution fusion | flops 67108864 | bytes 2637824 | tf_op jit(solution)/shard_map/dot_general | solution.py:39
  160.5 32.2 %all-gather.3.cloned.1.call-done = bf16[128,14336]{1,0:T(8,128)(2,1)} async-done(((bf16[128,1792]{1,0:T(8,128)(2,1)}), bf16[128,14336]{1,0:T(8,128)(2,1)}) %all-gather.3.cloned.1.call-update) | async-done | bytes 3670032 | tf_op jit(solution)/shard_map/all_gather | solution.py:33
  192.6 0.0 copy-done
  192.7 3.9 %fusion.11 = f32[128]{0:T(128)} fusion(f32[32,128]{1,0:T(8,128)S(1)} %fusion.14, bf16[128,14336]{1,0:T(8,128)(2,1)} %all-gather.3.cloned.1.call-done, bf16[1,32,14336]{2,1,0:T(8,128)(2,1)S(1)} %copy-done), kind=kOutput, calls=%fused_computation.12 | convolution fusion | flops 117448576 | bytes 4604416 | tf_op jit(solution)/shard_map/dot_general | solution.py:31
  (1 shorter events, 0.0 us)
Async XLA Ops:
  7.4 185.3 %copy-start = (bf16[1,32,14336]{2,1,0:T(8,128)(2,1)S(1)}, bf16[1,32,14336]{2,1,0:T(8,128)(2,1)}, u32[]{:S(2)}) copy-start(bf16[1,32,14336]{2,1,0:T(8,128)(2,1)} %param.12) | copy-start | bytes 2752516
  7.4 4.4 %copy-start.2 = (f32[8192]{0:T(1024)S(1)}, f32[8192]{0:T(1024)}, u32[]{:S(2)}) copy-start(f32[8192]{0:T(1024)} %param.8) | copy-start | bytes 98308
  7.4 148.2 %reduce-scatter.2.cloned.1.call-start = ((), (), s32[]{:S(2)}) async-start(), calls=%async_computation.2 | async-start | bytes 4587520 | tf_op jit(solution)/shard_map/reduce_scatter | solution.py:17
  87.7 70.4 %copy-start.1 = (bf16[1,32,8192]{2,1,0:T(8,128)(2,1)S(1)}, bf16[1,32,8192]{2,1,0:T(8,128)(2,1)}, u32[]{:S(2)}) copy-start(bf16[1,32,8192]{2,1,0:T(8,128)(2,1)} %param.13) | copy-start | bytes 1572868
  87.7 70.4 %all-gather.5.cloned.1.call-start = ((), (), s32[]{:S(2)}) async-start(), calls=%async_computation.4 | async-start | bytes 2359296 | tf_op jit(solution)/shard_map/all_gather | solution.py:41
  88.3 104.4 %all-gather.3.cloned.1.call-start = ((), (), s32[]{:S(2)}) async-start(), calls=%async_computation.3 | async-start | bytes 4128768 | tf_op jit(solution)/shard_map/all_gather | solution.py:33
Sparse Core Ops, SparseCore 0:
  87.8 67.7 reduce-scatter.1
Sparse Core Ops, SparseCore 1:
  90.1 26.9 all-gather.4
  158.1 34.5 all-gather.2
where the time goes:
time: 204 us
  waiting for transfers between devices  100 us (49%)
  blocking collectives  54.3 us (27%)
  matrix products  21.6 us (11%)
  between operations  14.9 us (7%)
  other arithmetic  6.99 us (3%)
  local copies, waits for them, and re-layouts  6 us (3%)
    reduce_scatter x1, waiting for transfers between devices, on_device(): lax.psum_scatter(jnp.dot(all_rows, paired, preferred_element_type=jnp.flo...  67.3 us
    all_to_all x1, blocking collectives, on_device(): lax.all_to_all(normed, 'train', split_axis=1, concat_axis=0, tiled=True)  54.3 us
    all_gather x1, waiting for transfers between devices, on_device(): lax.all_gather(activation, ('query', 'mp'), axis=1, tiled=True)  32.2 us
    dot_general x1, matrix products, on_device(): jnp.dot(all_rows, paired, preferred_element_type=jnp.float32)  15.3 us
  transfers between devices with their start and end apart: 3, of which 2 were waited for; matrix products, arithmetic and copies ran while one was open for 2% of the time, Pallas kernels for 0%

commit v1 on v0

--- a/solution.py
+++ b/solution.py
@@ -12,7 +12,10 @@
     normed = (values * lax.rsqrt(mean_sq + norm_eps) * norm_gain[None, :]).astype(jnp.bfloat16)
     tok_rows = normed.shape[0]
     hidden_cols = gate_weight.shape[1]
-    all_rows = lax.all_to_all(normed, "train", split_axis=1, concat_axis=0, tiled=True)
+    all_rows = jnp.concatenate(
+        lax.all_to_all(jnp.stack(jnp.split(normed, lax.axis_size("train"), axis=1)), "train", 0, 0),
+        axis=0,
+    )
     paired = jnp.concatenate([gate_weight, up_weight], axis=1)
     summed = lax.psum_scatter(
         jnp.dot(all_rows, paired, preferred_element_type=jnp.float32).astype(jnp.bfloat16),

time: 204 us -> 198 us (0.971)
  local copies, waits for them, and re-layouts: 6 us -> 0.25 us
    unnamed x7 -> x4, local copies, waits for them, and re-layouts: 3.32 us -> 0.01 us
    all_to_all x1 -> x0, local copies, waits for them, and re-layouts: 2.68 us -> none  [on_device(): lax.all_to_all(normed, 'train', split_axis=1, concat_axis=0, tiled=True)]
where the time goes in v1:
time: 198 us
  waiting for transfers between devices  100 us (51%)
  blocking collectives  54.3 us (27%)
  matrix products  21 us (11%)
  between operations  14.9 us (8%)
  other arithmetic  7 us (4%)
    reduce_scatter x1, waiting for transfers between devices, on_device(): lax.psum_scatter(jnp.dot(all_rows, paired, preferred_element_type=jnp.flo...  67.3 us
    all_to_all x1, blocking collectives, on_device(): lax.all_to_all(jnp.stack(jnp.split(normed, lax.axis_size('train'), axis=1...  54.3 us
    all_gather x1, waiting for transfers between devices, on_device(): lax.all_gather(activation, ('query', 'mp'), axis=1, tiled=True)  32.1 us
    dot_general x1, matrix products, on_device(): jnp.dot(all_rows, paired, preferred_element_type=jnp.float32)  14.7 us
  transfers between devices with their start and end apart: 3, of which 2 were waited for; matrix products, arithmetic and copies ran while one was open for 2% of the time, Pallas kernels for 0%

profile of v1, /device:TPU:0, one launch (start us, length us, event | category | flops | bytes accessed | tf_op | source)
XLA Modules:
  0.0 197.6 jit_solution(10406666988058493172)
XLA Ops:
  7.4 0.0 copy-start
  7.4 0.0 reduce-scatter.2.cloned.1.call-start
  7.4 2.2 %fusion.7 = f32[128]{0:T(128)S(1)} fusion(bf16[128,8192]{1,0:T(8,128)(2,1)} %param.7), kind=kLoop, calls=%fused_computation.7 | loop fusion | flops 3145600 | bytes 2097664 | tf_op jit(solution)/shard_map/reduce_sum | solution.py:11
  9.5 2.2 %fusion.9 = bf16[128,8192]{1,0:T(8,128)(2,1)S(1)} fusion(bf16[128,8192]{1,0:T(8,128)(2,1)} %param.7, f32[8192]{0:T(1024)} %param.8, f32[128]{0:T(128)S(1)} %add_rsqrt_fusion), kind=kLoop, calls=%fused_computation.9 | loop fusion | flops 4194304 | bytes 4227584 | tf_op jit(solution)/shard_map/convert_element_type | solution.py:12
  11.7 0.2 slice_bitcast_fusion.3
  12.0 0.3 pad_maximum_fusion
  12.2 54.3 %all_to_all.5 = bf16[4,128,2048]{2,1,0:T(8,128)(2,1)S(1)} all-to-all(bf16[4,128,2048]{2,1,0:T(8,128)(2,1)S(1)} %pad_maximum_fusion), channel_id=1, replica_groups=mesh['query'=4,'train'=4,'mp'=2] {'train'}, dimensions={0} | all-to-all | bytes 4194304 | tf_op jit(solution)/shard_map/all_to_all | solution.py:16
  66.6 14.7 %fusion.4 = bf16[512,3584]{1,0:T(8,128)(2,1)} fusion(bf16[512,2048]{1,0:T(8,128)(2,1)S(1)} %bitcast.25, bf16[2048,1792]{1,0:T(8,128)(2,1)} %param.10, bf16[2048,1792]{1,0:T(8,128)(2,1)} %param.9), kind=kOutput, calls=%fused_computation.4 | convolution fusion | flops 7547387904 | bytes 20447232 | tf_op jit(solution)/shard_map/dot_general | solution.py:21
  81.3 0.0 reduce-scatter.2.cloned.1.call-update
  81.3 0.0 copy-start.1
  81.3 0.0 all-gather.5.cloned.1.call-start
  81.4 0.5 all-gather.5.cloned.1.call-update
  81.9 0.0 all-gather.3.cloned.1.call-start
  82.0 67.3 %reduce-scatter.2.cloned.1.call-done = bf16[128,3584]{1,0:T(8,128)(2,1)} async-done(((bf16[512,3584]{1,0:T(8,128)(2,1)}), bf16[128,3584]{1,0:T(8,128)(2,1)}) %reduce-scatter.2.cloned.1.call-update) | async-done | bytes 917520 | tf_op jit(solution)/shard_map/reduce_scatter | solution.py:20
  149.3 1.4 convert_element_type.18
  150.6 1.0 fusion.12
  151.7 0.0 all-gather.3.cloned.1.call-update
  151.7 0.0 all-gather.5.cloned.1.call-done
  151.7 0.0 copy-done.1
  151.7 2.4 %fusion.14 = f32[32,128]{1,0:T(8,128)S(1)} fusion(bf16[128,8192]{1,0:T(8,128)(2,1)} %all-gather.5.cloned.1.call-done, bf16[1,32,8192]{2,1,0:T(8,128)(2,1)S(1)} %copy-done.1), kind=kOutput, calls=%fused_computation.21 | convolution fusion | flops 67108864 | bytes 2637824 | tf_op jit(solution)/shard_map/dot_general | solution.py:42
  154.1 32.1 %all-gather.3.cloned.1.call-done = bf16[128,14336]{1,0:T(8,128)(2,1)} async-done(((bf16[128,1792]{1,0:T(8,128)(2,1)}), bf16[128,14336]{1,0:T(8,128)(2,1)}) %all-gather.3.cloned.1.call-update) | async-done | bytes 3670032 | tf_op jit(solution)/shard_map/all_gather | solution.py:36
  186.3 0.0 copy-done
  186.3 3.9 %fusion.11 = f32[128]{0:T(128)} fusion(f32[32,128]{1,0:T(8,128)S(1)} %fusion.14, bf16[128,14336]{1,0:T(8,128)(2,1)} %all-gather.3.cloned.1.call-done, bf16[1,32,14336]{2,1,0:T(8,128)(2,1)S(1)} %copy-done), kind=kOutput, calls=%fused_computation.13 | convolution fusion | flops 117448576 | bytes 4604416 | tf_op jit(solution)/shard_map/dot_general | solution.py:34
  (1 shorter events, 0.0 us)
Async XLA Ops:
  7.4 178.9 %copy-start = (bf16[1,32,14336]{2,1,0:T(8,128)(2,1)S(1)}, bf16[1,32,14336]{2,1,0:T(8,128)(2,1)}, u32[]{:S(2)}) copy-start(bf16[1,32,14336]{2,1,0:T(8,128)(2,1)} %param.12) | copy-start | bytes 2752516
  7.4 141.9 %reduce-scatter.2.cloned.1.call-start = ((), (), s32[]{:S(2)}) async-start(), calls=%async_computation.2 | async-start | bytes 4587520 | tf_op jit(solution)/shard_map/reduce_scatter | solution.py:20
  81.3 70.4 %copy-start.1 = (bf16[1,32,8192]{2,1,0:T(8,128)(2,1)S(1)}, bf16[1,32,8192]{2,1,0:T(8,128)(2,1)}, u32[]{:S(2)}) copy-start(bf16[1,32,8192]{2,1,0:T(8,128)(2,1)} %param.13) | copy-start | bytes 1572868
  81.3 70.4 %all-gather.5.cloned.1.call-start = ((), (), s32[]{:S(2)}) async-start(), calls=%async_computation.4 | async-start | bytes 2359296 | tf_op jit(solution)/shard_map/all_gather | solution.py:44
  81.9 104.4 %all-gather.3.cloned.1.call-start = ((), (), s32[]{:S(2)}) async-start(), calls=%async_computation.3 | async-start | bytes 4128768 | tf_op jit(solution)/shard_map/all_gather | solution.py:36
Sparse Core Ops, SparseCore 0:
  81.4 67.7 reduce-scatter.1
Sparse Core Ops, SparseCore 1:
  83.7 26.9 all-gather.4
  151.8 34.5 all-gather.2
